TPU v7x, 32 devices: a whole 2x2x4 slice. The times are simulated.
32 devices in a mesh: rep: 8 (over z, x), tp: 4 (over y, core).
Axes of the slice: x: 2, y: 2, z: 4, core: 2. Of those that a mesh axis runs over, the one named last changes fastest.
Arguments:
- stream_in: bfloat16 [32, 4, 8192], P('rep', None, 'tp'), may hold values from -6 to 6
- queries: bfloat16 [32, 4, 4096], P('rep'), may hold values from -90 to 90
- new_keys: bfloat16 [32, 4, 4, 128], P('rep'), may hold values from -4 to 4
- new_values: bfloat16 [32, 4, 4, 128], P('rep'), may hold values from -4 to 4
- key_cache: bfloat16 [32, 1024, 4, 128], P('rep', 'tp'), may hold values from -4.1 to 4.1
- value_cache: bfloat16 [32, 1024, 4, 128], P('rep', 'tp'), may hold values from -4 to 4
- lengths: int32 [32], P('rep'), may hold values from 2 to 1024
- out_weight: bfloat16 [4096, 8192], P('tp', 'rep'), may hold values from -0.09375 to 0.09375
- norm_gain: bfloat16 [8192], P('tp'), may hold values from 0.5 to 1.5
Outputs:
- stream_out: bfloat16 [32, 4, 8192], P('rep', None, 'tp')
- normed: bfloat16 [32, 4, 8192], P('rep', None, 'tp')
All inputs are finite; a program needn't handle non-finite values.
Results may differ from a plain program's by a relative error of at most 0.0065.
Values may be sent and summed in bfloat16 or wider, within the bound.
A program may use at most 64 MiB of HBM per device.

v0:
```python
import math
import jax
import jax.numpy as jnp
from jax import lax
from jax.sharding import PartitionSpec as P

D = 8192


def on_device(
    stream_in, queries, new_keys, new_values, key_cache, value_cache, lengths, out_weight, norm_gain
):
    row_count, step_count, width = queries.shape
    kv_heads, head_dim = (key_cache.shape[2], key_cache.shape[3])
    block_len = key_cache.shape[1]
    group_size = width // head_dim // kv_heads
    tp_index = lax.axis_index("tp")
    scaling = 1.0 / math.sqrt(head_dim)
    grouped = queries.reshape(row_count, step_count, kv_heads, group_size, head_dim)
    cached = (
        jnp.einsum("bsgjd,bpgd->bsgjp", grouped, key_cache, preferred_element_type=jnp.float32)
        * scaling
    )
    positions = tp_index * block_len + jnp.arange(block_len, dtype=jnp.int32)
    visible = positions[None, :] < lengths[:, None]
    cached = jnp.where(visible[:, None, None, None, :], cached, -1e30)
    fresh = (
        jnp.einsum("bsgjd,btgd->bsgjt", grouped, new_keys, preferred_element_type=jnp.float32)
        * scaling
    )
    causal = (jnp.arange(step_count)[None, :] <= jnp.arange(step_count)[:, None]) & (tp_index == 0)
    fresh = jnp.where(causal[None, :, None, None, :], fresh, -1e30)
    local_maxima = jnp.maximum(cached.max(-1), fresh.max(-1))
    maxima = lax.pmax(local_maxima, "tp")
    weights_cached = jnp.exp(cached - maxima[..., None])
    weights_fresh = jnp.exp(fresh - maxima[..., None])
    denominator = weights_cached.sum(-1) + weights_fresh.sum(-1)
    numerator = jnp.einsum(
        "bsgjp,bpgd->bsgjd",
        weights_cached.astype(jnp.bfloat16),
        value_cache,
        preferred_element_type=jnp.float32,
    )
    numerator = numerator + jnp.einsum(
        "bsgjt,btgd->bsgjd",
        weights_fresh.astype(jnp.bfloat16),
        new_values,
        preferred_element_type=jnp.float32,
    )
    numerator = numerator.reshape(row_count, step_count, kv_heads * group_size, head_dim)
    denominator = denominator.reshape(row_count, step_count, kv_heads * group_size)
    numerator, denominator = (
        lax.psum_scatter(
            numerator.astype(jnp.bfloat16), "tp", scatter_dimension=2, tiled=True
        ).astype(jnp.float32),
        lax.psum_scatter(
            denominator.astype(jnp.bfloat16), "tp", scatter_dimension=2, tiled=True
        ).astype(jnp.float32),
    )
    attended = (numerator / denominator[..., None]).astype(jnp.bfloat16)
    attended = attended.reshape(row_count * step_count, -1)
    projected = jnp.dot(
        lax.all_gather(attended, "rep", axis=0, tiled=True),
        out_weight,
        preferred_element_type=jnp.float32,
    ).astype(jnp.bfloat16)
    partial_value = lax.all_to_all(
        projected, "rep", split_axis=0, concat_axis=1, tiled=True
    ).astype(jnp.float32)
    summed = lax.psum_scatter(
        partial_value.astype(jnp.bfloat16), "tp", scatter_dimension=1, tiled=True
    ).astype(jnp.float32)
    hidden = stream_in.reshape(row_count * step_count, -1).astype(jnp.float32) + summed
    squares = lax.psum(jnp.sum(hidden * hidden, axis=1), "tp")
    inverse = lax.rsqrt(squares / D + 1e-06)
    normed = hidden * inverse[:, None] * norm_gain.astype(jnp.float32)[None, :]
    stream_out = hidden.astype(jnp.bfloat16).reshape(row_count, step_count, -1)
    return (stream_out, normed.astype(jnp.bfloat16).reshape(row_count, step_count, -1))


def solution(mesh):
    return jax.shard_map(
        on_device,
        mesh=mesh,
        in_specs=(
            P("rep", None, "tp"),
            P("rep", None, None),
            P("rep", None, None, None),
            P("rep", None, None, None),
            P("rep", "tp", None, None),
            P("rep", "tp", None, None),
            P("rep"),
            P("tp", "rep"),
            P("tp"),
        ),
        out_specs=(P("rep", None, "tp"), P("rep", None, "tp")),
        check_vma=False,
    )
```

profile of v0, /device:TPU:0, one launch (start us, length us, event | category | flops | bytes accessed | tf_op | source)
XLA Modules:
  0.0 127.4 jit_solution(1407445413883382145)
XLA Ops:
  7.2 0.0 copy-start
  7.2 0.0 copy-start.4
  7.2 0.0 reduce-scatter.8.cloned.1.call-start
  7.2 1.2 reshape.73
  8.5 0.7 broadcast_compare_fusion
  9.2 0.0 copy-start.2
  9.2 1.8 %fusion.23 = (f32[4,4,4,8]{3,1,2,0:T(4,128)S(1)}, f32[4,4,4,8,256]{4,3,1,2,0:T(8,128)S(1)}) fusion(bf16[4,4,4,8,128]{4,3,2,1,0:T(8,128)(2,1)S(1)} %reshape.73, bf16[4,256,4,128,1]{3,2,1,0,4:T(4,128)(2,1)} %bitcast.43, pred[4,256]{1,0:T(4,128)(4,1)S(1)} %broadcast_compare_fusion), kind=kOutput, calls=%fused_computation.40 | convolution fusion | flops 33947136 | bytes 1707008 | tf_op jit(solution)/shard_map/bsgjd,bpgd->bsgjp/dot_general | solution.py:21
  11.0 0.0 copy-done.4
  11.0 0.7 fusion.24
  11.7 12.9 %pmax.7 = f32[4,4,4,8]{3,1,2,0:T(4,128)S(1)} all-reduce(f32[4,4,4,8]{3,1,2,0:T(4,128)S(1)} %max.5), channel_id=1, replica_groups=mesh['rep'=8,'tp'=4] {'tp'}, use_global_device_ids=true, to_apply=%region_2.3 | all-reduce | flops 512 | bytes 4096 | tf_op jit(solution)/shard_map/pmax | solution.py:34
  24.7 0.0 copy-start.5
  24.7 1.5 %fusion.6 = f32[4,4,4,8,128]{4,3,2,1,0:T(8,128)S(1)} fusion(bf16[4,256,4,128,1]{3,2,1,0,4:T(4,128)(2,1)} %bitcast.33, f32[4,4,4,8,256]{4,3,1,2,0:T(8,128)S(1)} %get-tuple-element.5, f32[4,4,4,8]{3,1,2,0:T(4,128)S(1)} %pmax.7), kind=kOutput, calls=%fused_computation.10 | convolution fusion | flops 33816576 | bytes 1837056 | tf_op jit(solution)/shard_map/bsgjp,bpgd->bsgjd/dot_general | solution.py:38
  26.2 0.0 copy-done.2
  26.2 0.3 fusion.3
  26.5 0.1 copy.84
  26.6 0.7 reshape.82
  27.3 0.0 reduce-scatter.8.cloned.1.call-update
  27.3 0.0 reduce-scatter.6.cloned.1.call-start
  27.4 0.3 fusion.9
  27.7 0.1 fusion.15
  27.9 0.1 convert_element_type.62
  27.9 0.0 copy-done.5
  27.9 0.6 dynamic-slice
  29.2 5.8 %all-reduce = bf16[4,4,32]{2,1,0:T(4,128)(2,1)S(1)} all-reduce(bf16[4,4,32]{2,1,0:T(4,128)(2,1)S(1)} %convert_element_type.62), channel_id=3, replica_groups=mesh['rep'=8,'tp'=4] {'tp'}, use_global_device_ids=true, to_apply=%region_6.7.clone | all-reduce | flops 512 | bytes 2048
  35.0 0.1 dynamic-slice_convert_fusion
  35.0 12.4 %reduce-scatter.8.cloned.1.call-done = bf16[8,2048]{1,0:T(8,128)(2,1)} async-done(((bf16[32,2048]{1,0:T(8,128)(2,1)}), bf16[8,2048]{1,0:T(8,128)(2,1)}) %reduce-scatter.8.cloned.1.call-update) | async-done | bytes 32784
  47.4 0.8 reshape.83
  48.2 0.1 divide_convert_fusion
  48.3 0.0 copy-start.1
  48.3 30.9 %all_gather.3 = bf16[128,1024]{1,0:T(8,128)(2,1)S(1)} all-gather(bf16[16,1024]{1,0:T(8,128)(2,1)S(1)} %bitcast.39), channel_id=1, replica_groups=mesh['rep'=8,'tp'=4] {'rep'}, dimensions={0}, use_global_device_ids=true | all-gather | bytes 294912 | tf_op jit(solution)/shard_map/all_gather | solution.py:63
  79.2 0.0 copy-done
  79.2 0.0 copy-start.3
  79.2 0.4 convolution_convert_fusion
  79.7 13.5 %all_to_all.19 = bf16[8,16,1024]{2,1,0:T(8,128)(2,1)S(1)} all-to-all(bf16[8,16,1024]{2,1,0:T(8,128)(2,1)S(1)} %bitcast.34), channel_id=1, replica_groups=mesh['rep'=8,'tp'=4] {'rep'}, dimensions={0} | all-to-all | bytes 524288 | tf_op jit(solution)/shard_map/all_to_all | solution.py:67
  93.2 0.7 copy.58
  93.9 0.0 reduce-scatter.6.cloned.1.call-update
  93.9 0.0 copy-done.1
  94.0 0.0 copy-done.3
  94.0 17.5 %reduce-scatter.6.cloned.1.call-done = bf16[16,2048]{1,0:T(8,128)(2,1)} async-done(((bf16[16,8192]{1,0:T(8,128)(2,1)}), bf16[16,2048]{1,0:T(8,128)(2,1)}) %reduce-scatter.6.cloned.1.call-update) | async-done | bytes 65552 | tf_op jit(solution)/shard_map/reduce_scatter | solution.py:70
  111.5 1.0 multiply_reduce_fusion
  112.5 5.8 %psum.7 = f32[16]{0:T(128)S(1)} all-reduce(f32[16]{0:T(128)S(1)} %multiply_reduce_fusion), channel_id=1, replica_groups=mesh['rep'=8,'tp'=4] {'tp'}, use_global_device_ids=true, to_apply=%region_9.10 | all-reduce | flops 16 | bytes 128 | tf_op jit(solution)/shard_map/psum | solution.py:74
  118.3 0.9 multiply_convert_fusion
  119.2 0.7 reshape.75
  119.9 0.7 reshape.76
  (10 shorter events, 0.1 us)
Async XLA Ops:
  7.2 72.1 %copy-start = (bf16[1024,1024]{1,0:T(8,128)(2,1)S(1)}, bf16[1024,1024]{1,0:T(8,128)(2,1)}, u32[]{:S(2)}) copy-start(bf16[1024,1024]{1,0:T(8,128)(2,1)} %param.16) | copy-start | bytes 6291460
  7.2 3.8 %copy-start.4 = (bf16[4,4,4,128]{3,2,1,0:T(4,128)(2,1)S(1)}, bf16[4,4,4,128]{3,2,1,0:T(4,128)(2,1)}, u32[]{:S(2)}) copy-start(bf16[4,4,4,128]{3,2,1,0:T(4,128)(2,1)} %param.11) | copy-start | bytes 49156
  7.2 40.2 %reduce-scatter.8.cloned.1.call-start = ((), (), s32[]{:S(2)}) async-start(), calls=%async_computation.4 | async-start | bytes 163840
  9.2 17.0 %copy-start.2 = (bf16[4,4,4,128]{3,2,1,0:T(4,128)(2,1)S(1)}, bf16[4,4,4,128]{3,2,1,0:T(4,128)(2,1)}, u32[]{:S(2)}) copy-start(bf16[4,4,4,128]{3,2,1,0:T(4,128)(2,1)} %param.12) | copy-start | bytes 49156
  24.7 3.3 %copy-start.5 = (u32[32]{0:T(128)S(1)}, u32[32]{0:T(128)}, u32[]{:S(2)}) copy-start(u32[32]{0:T(128)} %constant.31) | copy-start | bytes 388
  27.3 84.2 %reduce-scatter.6.cloned.1.call-start = ((), (), s32[]{:S(2)}) async-start(), calls=%async_computation.3 | async-start | bytes 327680 | tf_op jit(solution)/shard_map/reduce_scatter | solution.py:70
  48.3 45.6 %copy-start.1 = (bf16[4,4,2048]{2,1,0:T(4,128)(2,1)S(1)}, bf16[4,4,2048]{2,1,0:T(4,128)(2,1)}, u32[]{:S(2)}) copy-start(bf16[4,4,2048]{2,1,0:T(4,128)(2,1)} %param.9) | copy-start | bytes 196612
  79.2 14.7 %copy-start.3 = (bf16[2048]{0:T(1024)(128)(2,1)S(1)}, bf16[2048]{0:T(1024)(128)(2,1)}, u32[]{:S(2)}) copy-start(bf16[2048]{0:T(1024)(128)(2,1)} %param.17) | copy-start | bytes 12292
Sparse Core Ops, SparseCore 0:
  27.4 19.9 reduce-scatter.7
  94.1 17.4 reduce-scatter.5
where the time goes:
time: 128 us; the launch traced here: 127 us
  blocking collectives  68.9 us (54%)
  waiting for transfers between devices  29.9 us (23%)
  between operations  14.9 us (12%)
  local copies, waits for them, and re-layouts  5.54 us (4%)
  matrix products  4.72 us (4%)
  other arithmetic  3.27 us (3%)
    all_gather x1, blocking collectives, on_device(): lax.all_gather(attended, 'rep', axis=0, tiled=True)  30.9 us
    reduce_scatter x1, waiting for transfers between devices, on_device(): lax.psum_scatter(partial_value.astype(jnp.bfloat16), 'tp', scatter_dimens...  17.5 us
    all_to_all x1, blocking collectives, on_device(): lax.all_to_all(projected, 'rep', split_axis=0, concat_axis=1, tiled=True)  13.5 us
    pmax x1, blocking collectives, on_device(): maxima = lax.pmax(local_maxima, 'tp')  12.9 us
    unnamed x3, waiting for transfers between devices  12.4 us
    unnamed x1, blocking collectives  5.77 us
    psum x1, blocking collectives, on_device(): squares = lax.psum(jnp.sum(hidden * hidden, axis=1), 'tp')  5.76 us
  transfers between devices with their start and end apart: 2, of which 2 were waited for; matrix products, arithmetic and copies ran while one was open for 1% of the time, Pallas kernels for 0%

commit v1 on v0

--- a/solution.py
+++ b/solution.py
@@ -60,7 +60,9 @@
     attended = (numerator / denominator[..., None]).astype(jnp.bfloat16)
     attended = attended.reshape(row_count * step_count, -1)
     projected = jnp.dot(
-        lax.all_gather(attended, "rep", axis=0, tiled=True),
+        jnp.concatenate(
+            lax.all_to_all(jnp.stack([attended] * lax.axis_size("rep")), "rep", 0, 0), axis=0
+        ),
         out_weight,
         preferred_element_type=jnp.float32,
     ).astype(jnp.bfloat16)

time: 128 us -> 110 us (0.86)
  blocking collectives: 68.9 us -> 50 us
    all_gather x1 -> x0, blocking collectives: 30.9 us -> none  [on_device(): lax.all_gather(attended, 'rep', axis=0, tiled=True)]
    all_to_all x0 -> x1, blocking collectives: none -> 13.8 us  [on_device(): lax.all_to_all(jnp.stack([attended] * lax.axis_size('rep')), 'rep', 0, 0)]
    all_to_all x1, blocking collectives: 13.5 us -> 11.8 us  [on_device(): lax.all_to_all(projected, 'rep', split_axis=0, concat_axis=1, tiled=True)]
where the time goes in v1:
time: 110 us; the launch traced here: 109 us
  blocking collectives  50 us (45%)
  waiting for transfers between devices  30.6 us (28%)
  between operations  14.9 us (14%)
  local copies, waits for them, and re-layouts  5.56 us (5%)
  matrix products  4.72 us (4%)
  other arithmetic  3.27 us (3%)
    reduce_scatter x1, waiting for transfers between devices, on_device(): lax.psum_scatter(partial_value.astype(jnp.bfloat16), 'tp', scatter_dimens...  18.2 us
    all_to_all x1, blocking collectives, on_device(): lax.all_to_all(jnp.stack([attended] * lax.axis_size('rep')), 'rep', 0, 0)  13.8 us
    pmax x1, blocking collectives, on_device(): maxima = lax.pmax(local_maxima, 'tp')  12.9 us
    unnamed x3, waiting for transfers between devices  12.4 us
    all_to_all x1, blocking collectives, on_device(): lax.all_to_all(projected, 'rep', split_axis=0, concat_axis=1, tiled=True)  11.8 us
    unnamed x1, blocking collectives  5.77 us
    psum x1, blocking collectives, on_device(): squares = lax.psum(jnp.sum(hidden * hidden, axis=1), 'tp')  5.76 us
  transfers between devices with their start and end apart: 2, of which 2 were waited for; matrix products, arithmetic and copies ran while one was open for 1% of the time, Pallas kernels for 0%

profile of v1, /device:TPU:0, one launch (start us, length us, event | category | flops | bytes accessed | tf_op | source)
XLA Modules:
  0.0 109.2 jit_solution(9250707256580217124)
XLA Ops:
  7.2 0.0 copy-start
  7.2 0.0 copy-start.4
  7.2 0.0 reduce-scatter.8.cloned.1.call-start
  7.2 1.2 %reshape.75 = bf16[4,4,4,8,128]{4,3,2,1,0:T(8,128)(2,1)S(1)} reshape(bf16[4,4,4096]{2,1,0:T(4,128)(2,1)} %param.10) | data formatting | bytes 262144 | tf_op jit(solution)/shard_map/reshape | solution.py:19
  8.5 0.7 broadcast_compare_fusion
  9.2 0.0 copy-start.2
  9.2 1.8 %fusion.23 = (f32[4,4,4,8]{3,1,2,0:T(4,128)S(1)}, f32[4,4,4,8,256]{4,3,1,2,0:T(8,128)S(1)}) fusion(bf16[4,4,4,8,128]{4,3,2,1,0:T(8,128)(2,1)S(1)} %reshape.75, bf16[4,256,4,128,1]{3,2,1,0,4:T(4,128)(2,1)} %bitcast.45, pred[4,256]{1,0:T(4,128)(4,1)S(1)} %broadcast_compare_fusion), kind=kOutput, calls=%fused_computation.40 | convolution fusion | flops 33947136 | bytes 1707008 | tf_op jit(solution)/shard_map/bsgjd,bpgd->bsgjp/dot_general | solution.py:21
  11.0 0.0 copy-done.4
  11.0 0.7 fusion.24
  11.7 12.9 %pmax.7 = f32[4,4,4,8]{3,1,2,0:T(4,128)S(1)} all-reduce(f32[4,4,4,8]{3,1,2,0:T(4,128)S(1)} %max.5), channel_id=1, replica_groups=mesh['rep'=8,'tp'=4] {'tp'}, use_global_device_ids=true, to_apply=%region_2.3 | all-reduce | flops 512 | bytes 4096 | tf_op jit(solution)/shard_map/pmax | solution.py:34
  24.7 0.0 copy-start.5
  24.7 1.5 %fusion.6 = f32[4,4,4,8,128]{4,3,2,1,0:T(8,128)S(1)} fusion(bf16[4,256,4,128,1]{3,2,1,0,4:T(4,128)(2,1)} %bitcast.34, f32[4,4,4,8,256]{4,3,1,2,0:T(8,128)S(1)} %get-tuple-element.5, f32[4,4,4,8]{3,1,2,0:T(4,128)S(1)} %pmax.7), kind=kOutput, calls=%fused_computation.10 | convolution fusion | flops 33816576 | bytes 1837056 | tf_op jit(solution)/shard_map/bsgjp,bpgd->bsgjd/dot_general | solution.py:38
  26.2 0.0 copy-done.2
  26.2 0.3 fusion.3
  26.5 0.1 copy.84
  26.6 0.7 reshape.84
  27.3 0.0 reduce-scatter.8.cloned.1.call-update
  27.3 0.0 reduce-scatter.6.cloned.1.call-start
  27.4 0.3 fusion.9
  27.7 0.1 fusion.15
  27.9 0.1 convert_element_type.62
  27.9 0.0 copy-done.5
  27.9 0.6 dynamic-slice
  29.2 5.8 %all-reduce = bf16[4,4,32]{2,1,0:T(4,128)(2,1)S(1)} all-reduce(bf16[4,4,32]{2,1,0:T(4,128)(2,1)S(1)} %convert_element_type.62), channel_id=3, replica_groups=mesh['rep'=8,'tp'=4] {'tp'}, use_global_device_ids=true, to_apply=%region_6.7.clone | all-reduce | flops 512 | bytes 2048
  35.0 0.1 dynamic-slice_convert_fusion
  35.0 12.4 %reduce-scatter.8.cloned.1.call-done = bf16[8,2048]{1,0:T(8,128)(2,1)} async-done(((bf16[32,2048]{1,0:T(8,128)(2,1)}), bf16[8,2048]{1,0:T(8,128)(2,1)}) %reduce-scatter.8.cloned.1.call-update) | async-done | bytes 32784
  47.4 0.8 reshape.85
  48.2 0.1 divide_convert_fusion
  48.3 13.8 %all_to_all.24 = bf16[8,16,1024]{2,1,0:T(8,128)(2,1)S(1)} all-to-all(bf16[8,16,1024]{2,1,0:T(8,128)(2,1)S(1)} %stack.3), channel_id=1, replica_groups=mesh['rep'=8,'tp'=4] {'rep'}, dimensions={0} | all-to-all | bytes 524288 | tf_op jit(solution)/shard_map/all_to_all | solution.py:64
  62.1 0.0 copy-start.1
  62.1 0.0 copy-start.3
  62.1 0.0 copy-done
  62.1 0.4 convolution_convert_fusion
  62.6 11.8 %all_to_all.25 = bf16[8,16,1024]{2,1,0:T(8,128)(2,1)S(1)} all-to-all(bf16[8,16,1024]{2,1,0:T(8,128)(2,1)S(1)} %bitcast.36), channel_id=1, replica_groups=mesh['rep'=8,'tp'=4] {'rep'}, dimensions={0} | all-to-all | bytes 524288 | tf_op jit(solution)/shard_map/all_to_all | solution.py:69
  74.4 0.7 copy.58
  75.1 0.0 reduce-scatter.6.cloned.1.call-update
  75.1 0.0 copy-done.1
  75.1 0.0 copy-done.3
  75.2 18.2 %reduce-scatter.6.cloned.1.call-done = bf16[16,2048]{1,0:T(8,128)(2,1)} async-done(((bf16[16,8192]{1,0:T(8,128)(2,1)}), bf16[16,2048]{1,0:T(8,128)(2,1)}) %reduce-scatter.6.cloned.1.call-update) | async-done | bytes 65552 | tf_op jit(solution)/shard_map/reduce_scatter | solution.py:72
  93.3 1.0 multiply_reduce_fusion
  94.3 5.8 %psum.7 = f32[16]{0:T(128)S(1)} all-reduce(f32[16]{0:T(128)S(1)} %multiply_reduce_fusion), channel_id=1, replica_groups=mesh['rep'=8,'tp'=4] {'tp'}, use_global_device_ids=true, to_apply=%region_9.10 | all-reduce | flops 16 | bytes 128 | tf_op jit(solution)/shard_map/psum | solution.py:76
  100.1 0.9 multiply_convert_fusion
  101.0 0.7 reshape.77
  101.7 0.7 reshape.78
  (11 shorter events, 0.1 us)
Async XLA Ops:
  7.2 55.0 %copy-start = (bf16[1024,1024]{1,0:T(8,128)(2,1)S(1)}, bf16[1024,1024]{1,0:T(8,128)(2,1)}, u32[]{:S(2)}) copy-start(bf16[1024,1024]{1,0:T(8,128)(2,1)} %param.16) | copy-start | bytes 6291460
  7.2 3.8 %copy-start.4 = (bf16[4,4,4,128]{3,2,1,0:T(4,128)(2,1)S(1)}, bf16[4,4,4,128]{3,2,1,0:T(4,128)(2,1)}, u32[]{:S(2)}) copy-start(bf16[4,4,4,128]{3,2,1,0:T(4,128)(2,1)} %param.11) | copy-start | bytes 49156
  7.2 40.2 %reduce-scatter.8.cloned.1.call-start = ((), (), s32[]{:S(2)}) async-start(), calls=%async_computation.5 | async-start | bytes 163840
  9.2 17.0 %copy-start.2 = (bf16[4,4,4,128]{3,2,1,0:T(4,128)(2,1)S(1)}, bf16[4,4,4,128]{3,2,1,0:T(4,128)(2,1)}, u32[]{:S(2)}) copy-start(bf16[4,4,4,128]{3,2,1,0:T(4,128)(2,1)} %param.12) | copy-start | bytes 49156
  24.7 3.3 %copy-start.5 = (u32[32]{0:T(128)S(1)}, u32[32]{0:T(128)}, u32[]{:S(2)}) copy-start(u32[32]{0:T(128)} %constant.31) | copy-start | bytes 388
  27.3 66.0 %reduce-scatter.6.cloned.1.call-start = ((), (), s32[]{:S(2)}) async-start(), calls=%async_computation.4 | async-start | bytes 327680 | tf_op jit(solution)/shard_map/reduce_scatter | solution.py:72
  62.1 13.0 %copy-start.1 = (bf16[4,4,2048]{2,1,0:T(4,128)(2,1)S(1)}, bf16[4,4,2048]{2,1,0:T(4,128)(2,1)}, u32[]{:S(2)}) copy-start(bf16[4,4,2048]{2,1,0:T(4,128)(2,1)} %param.9) | copy-start | bytes 196612
  62.1 13.0 %copy-start.3 = (bf16[2048]{0:T(1024)(128)(2,1)S(1)}, bf16[2048]{0:T(1024)(128)(2,1)}, u32[]{:S(2)}) copy-start(bf16[2048]{0:T(1024)(128)(2,1)} %param.17) | copy-start | bytes 12292
Sparse Core Ops, SparseCore 0:
  27.4 19.9 reduce-scatter.7
  75.2 18.0 reduce-scatter.5
